TPU v7x, 32 devices: a whole 2x2x4 slice. The times are simulated.
32 devices in a mesh: dp: 8 (over z, y), expert: 2 (over x), tensor: 2 (over core).
Axes of the slice: x: 2, y: 2, z: 4, core: 2. Of those that a mesh axis runs over, the one named last changes fastest.
Arguments:
- tokens: bfloat16 [512, 4096], P('dp', 'tensor'), may hold values from -6 to 6
- targets: bfloat16 [512, 4096], P('dp', 'tensor'), may hold values from -6 to 6
- norm_gain: float32 [4096], P('tensor'), may hold values from 0.1 to 1.9
- expert_ids: int32 [512, 2], P('dp'), may hold values from 0 to 7, all different within a row; in each aligned block of 64 rows (0 to 63, 64 to 127, ...) at most 18 rows name the same one
- gate_prob: float32 [512, 2], P('dp'), may hold values from 0.2 to 1
- w_gate: bfloat16 [4096, 65536], P('tensor', ('dp', 'expert')), may hold values from -0.09375 to 0.09375
- gate_probe: bfloat16 [4096, 65536], P('tensor', ('dp', 'expert')), as said below
- w_up: bfloat16 [4096, 65536], P('tensor', ('dp', 'expert')), may hold values from -0.09375 to 0.09375
- w_down: bfloat16 [65536, 4096], P(('dp', 'expert'), 'tensor'), may hold values from -0.0625 to 0.0625
Outputs:
- normed: bfloat16 [512, 4096], P('dp', 'tensor')
- curvature: float32 [512, 2], P('dp')
- estimate: float32 [8], replicated
Inputs may be any that keep to these rules, and one draw needn't show every extreme that they name: `expert_ids`: the two ids of a token differ; within each block of 64 consecutive tokens no expert is named more than 18 times; every expert is named by some token. `gate_probe`: every entry is plus or minus 1 / sqrt(4096).
All inputs are finite; a program needn't handle non-finite values.
Results may differ from a plain program's by a relative error of at most 0.03.
Values may be sent and summed in bfloat16 or wider, within the bound.
No kernel may reach another device: no remote copies, remote signals or barrier semaphores. Data moves between devices by JAX's collectives and lax.ppermute only.
A program may use at most 128 MiB of HBM per device.

v0:
```python
import jax
import jax.numpy as jnp
from jax import lax
from jax.sharding import PartitionSpec as P

D = 4096
EXPERTS = 8
CAP = 18


epsilon = 1e-05
loss_weight = 8.0


def derivative_jets(preact):
    gate_in = preact[:, 0]
    gate_dir = preact[:, 1]
    up_in = preact[:, 2]
    sigmoid_in = jax.nn.sigmoid(gate_in)
    first_slope = sigmoid_in * (1.0 + gate_in * (1.0 - sigmoid_in))
    second_slope = sigmoid_in * (1.0 - sigmoid_in) * (2.0 + gate_in * (1.0 - 2.0 * sigmoid_in))
    primal = gate_in * sigmoid_in * up_in
    tangent = first_slope * gate_dir * up_in
    second = second_slope * gate_dir * gate_dir * up_in
    return jnp.stack([primal, tangent, second], axis=1).astype(jnp.bfloat16)


def slot_numbers(flat_ids):
    onehot = (flat_ids[:, None] == jnp.arange(EXPERTS, dtype=jnp.int32)[None, :]).astype(jnp.int32)
    before = jnp.cumsum(onehot, axis=0) - onehot
    return jnp.sum(before * onehot, axis=1)


def slot_curvature(inv_root, moments, weighted_uu, resid_b, resid_a, resid_u):
    inv_cube = inv_root * inv_root * inv_root
    first_rate = 2.0 * moments[..., 0] / D
    second_rate = 2.0 * (moments[..., 1] + moments[..., 2]) / D
    slope_one = -0.5 * inv_cube * first_rate
    slope_two = (
        0.75 * inv_cube * inv_root * inv_root * first_rate * first_rate
        - 0.5 * inv_cube * second_rate
    )
    tangent_sq = (
        inv_root * inv_root * moments[..., 3]
        + 2.0 * inv_root * slope_one * moments[..., 4]
        + slope_one * slope_one * weighted_uu
    )
    bending = inv_root * resid_b + 2.0 * slope_one * resid_a + slope_two * resid_u
    return 2.0 * loss_weight / D * (tangent_sq + bending)


def on_device(tokens, targets, norm_gain, expert_ids, gate_prob, w_gate, gate_probe, w_up, w_down):
    tok_rows, width_part = tokens.shape
    hidden_part = w_gate.shape[1]
    holders = lax.axis_size("dp") // EXPERTS
    flat_ids = expert_ids.reshape(-1)
    places = flat_ids * CAP + slot_numbers(flat_ids)
    outgoing = (
        jnp.zeros((EXPERTS * CAP, width_part), jnp.bfloat16)
        .at[places]
        .set(jnp.repeat(tokens, 2, axis=0))
    )
    outgoing = jnp.repeat(outgoing.reshape(EXPERTS, CAP, width_part), holders, axis=0)
    arrived = lax.all_to_all(outgoing, "dp", split_axis=0, concat_axis=0, tiled=True)
    senders = arrived.shape[0]
    expert_rows = arrived.reshape(senders * CAP, width_part)
    partial_value = jnp.stack(
        [
            jnp.dot(expert_rows, w_gate, preferred_element_type=jnp.float32),
            jnp.dot(expert_rows, gate_probe, preferred_element_type=jnp.float32),
            jnp.dot(expert_rows, w_up, preferred_element_type=jnp.float32),
        ],
        axis=1,
    )
    hidden_jets = derivative_jets(
        lax.psum(partial_value.astype(jnp.bfloat16), "tensor").astype(jnp.float32)
    )
    images = jnp.dot(
        hidden_jets.reshape(-1, hidden_part), w_down, preferred_element_type=jnp.float32
    )
    images = images.reshape(senders, CAP, 3, width_part).astype(jnp.bfloat16)
    halves = lax.psum_scatter(
        images.astype(jnp.float32).astype(jnp.bfloat16), "expert", scatter_dimension=3, tiled=True
    ).astype(jnp.float32)
    returned = lax.all_to_all(
        halves.astype(jnp.bfloat16), "dp", split_axis=0, concat_axis=0, tiled=True
    ).astype(halves.dtype)
    half_width = returned.shape[3]
    grouped = jnp.sum(returned.reshape(EXPERTS, holders, CAP, 3, half_width), axis=1)
    expert_table = lax.all_gather(
        grouped.astype(jnp.bfloat16), "expert", axis=3, tiled=True
    ).astype(grouped.dtype)
    picked = expert_table.reshape(EXPERTS * CAP, 3, width_part)[places].reshape(
        tok_rows, 2, 3, width_part
    )
    weights = gate_prob[:, :, None]
    summed = tokens.astype(jnp.float32) + jnp.sum(weights * picked[:, :, 0], axis=1)
    tangent_out = weights * picked[:, :, 1]
    second_out = weights * picked[:, :, 2]
    target = targets.astype(jnp.float32)
    gain_sq = norm_gain * norm_gain
    spread_sum = summed[:, None, :]
    cross_ua = jnp.sum(spread_sum * tangent_out, axis=-1)
    along_aa = jnp.sum(tangent_out * tangent_out, axis=-1)
    cross_ub = jnp.sum(spread_sum * second_out, axis=-1)
    weighted_aa = jnp.sum(gain_sq * tangent_out * tangent_out, axis=-1)
    weighted_au = jnp.sum(gain_sq * spread_sum * tangent_out, axis=-1)
    square_total = lax.psum(jnp.sum(summed * summed, axis=-1), "tensor")
    inv_root = lax.rsqrt(square_total / D + epsilon)[:, None]
    scaled = norm_gain * summed * inv_root
    residual = norm_gain * (scaled - target)
    slot_stats = jnp.stack(
        [
            cross_ua,
            along_aa,
            cross_ub,
            weighted_aa,
            weighted_au,
            jnp.sum(residual[:, None, :] * second_out, axis=-1),
            jnp.sum(residual[:, None, :] * tangent_out, axis=-1),
        ],
        axis=-1,
    )
    token_stats = jnp.stack(
        [jnp.sum(gain_sq * summed * summed, axis=-1), jnp.sum(residual * summed, axis=-1)], axis=-1
    )
    slot_total, token_total = lax.psum((slot_stats, token_stats), "tensor")
    weighted_uu = token_total[:, 0:1]
    resid_u = token_total[:, 1:2]
    resid_b = slot_total[..., 5]
    resid_a = slot_total[..., 6]
    normed = scaled.astype(jnp.bfloat16)
    curvature = slot_curvature(
        inv_root, slot_total[..., :5], weighted_uu, resid_b, resid_a, resid_u
    )
    member = (expert_ids[:, :, None] == jnp.arange(EXPERTS, dtype=jnp.int32)).astype(jnp.float32)
    totals, counts = lax.psum(
        (jnp.sum(member * curvature[:, :, None], axis=(0, 1)), jnp.sum(member, axis=(0, 1))), "dp"
    )
    return (normed, curvature, totals / counts)


def solution(mesh):
    return jax.shard_map(
        on_device,
        mesh=mesh,
        in_specs=(
            P("dp", "tensor"),
            P("dp", "tensor"),
            P("tensor"),
            P("dp", None),
            P("dp", None),
            P("tensor", ("dp", "expert")),
            P("tensor", ("dp", "expert")),
            P("tensor", ("dp", "expert")),
            P(("dp", "expert"), "tensor"),
        ),
        out_specs=(P("dp", "tensor"), P("dp", None), P()),
        check_vma=False,
    )
```

profile of v0, /device:TPU:0, one launch (start us, length us, event | category | flops | bytes accessed | tf_op | source)
XLA Modules:
  0.0 276.0 jit_solution(15197429949735670920)
XLA Ops:
  12.7 27.3 %all_to_all.10 = bf16[8,18,2048]{2,1,0:T(8,128)(2,1)S(1)} all-to-all(bf16[8,18,2048]{2,1,0:T(8,128)(2,1)S(1)} %reshape_broadcast_in_dim_reshape.3), channel_id=1, replica_groups=mesh['dp'=8,'expert'=2,'tensor'=2] {'dp'}, dimensions={0} | all-to-all | bytes 1179648 | tf_op jit(solution)/shard_map/all_to_all | solution.py:64
  40.1 8.5 %fusion.3 = bf16[144,1,4096]{2,0,1:T(8,128)(2,1)S(1)} fusion(bf16[144,2048]{1,0:T(8,128)(2,1)S(1)} %reshape.128, bf16[2048,4096]{1,0:T(8,128)(2,1)} %param.14), kind=kOutput, calls=%fused_computation.8 | convolution fusion | flops 2416508928 | bytes 18546688 | tf_op jit(solution)/shard_map/dot_general | solution.py:69
  48.7 2.0 copy-done
  50.7 2.8 fusion.4
  53.4 8.4 %fusion.5 = bf16[144,1,4096]{2,0,1:T(8,128)(2,1)S(1)} fusion(bf16[144,2048]{1,0:T(8,128)(2,1)S(1)} %reshape.128, bf16[2048,4096]{1,0:T(8,128)(2,1)} %param.16), kind=kOutput, calls=%fused_computation.10 | convolution fusion | flops 2416508928 | bytes 18546688 | tf_op jit(solution)/shard_map/dot_general | solution.py:71
  61.8 2.0 pad_maximum_fusion
  64.1 23.0 %all-reduce.4.cloned.1.call-done = bf16[144,3,4096]{2,0,1:T(8,128)(2,1)} async-done(((bf16[144,3,4096]{2,0,1:T(8,128)(2,1)}), bf16[144,3,4096]{2,0,1:T(8,128)(2,1)}) %all-reduce.4.cloned.1.call-update) | async-done | bytes 3538960 | tf_op jit(solution)/shard_map/psum | solution.py:76
  87.2 2.9 %convert_element_type.37 = f32[144,3,4096]{2,0,1:T(8,128)S(1)} convert(bf16[144,3,4096]{2,0,1:T(8,128)(2,1)} %all-reduce.4.cloned.1.call-done) | non-fusion elementwise | flops 1769472 | bytes 10616832 | tf_op jit(solution)/shard_map/convert_element_type | solution.py:76
  90.0 1.8 multiply_convert_fusion
  92.3 3.5 %convert_element_type.38 = bf16[8,18,3,4096]{3,1,0,2:T(8,128)(2,1)} reshape(bf16[144,3,4096]{2,0,1:T(8,128)(2,1)S(1)} %pad_maximum_fusion.1) | data formatting | bytes 7077888 | tf_op jit(solution)/shard_map/convert_element_type | solution.py:25
  95.8 15.9 %fusion.6 = bf16[8,18,3,2048]{3,1,2,0:T(8,128)(2,1)} fusion(bf16[4096,2048]{1,0:T(8,128)(2,1)} %param.17, bf16[8,18,3,4096]{3,1,0,2:T(8,128)(2,1)} %convert_element_type.38), kind=kOutput, calls=%fused_computation.16 | convolution fusion | flops 7248642048 | bytes 22085632 | tf_op jit(solution)/shard_map/dot_general | solution.py:78
  111.8 36.1 %reduce-scatter.2.cloned.1.call-done = bf16[8,18,3,1024]{3,1,2,0:T(8,128)(2,1)} async-done(((bf16[8,18,3,2048]{3,1,2,0:T(8,128)(2,1)}), bf16[8,18,3,1024]{3,1,2,0:T(8,128)(2,1)}) %reduce-scatter.2.cloned.1.call-update) | async-done | bytes 884752 | tf_op jit(solution)/shard_map/reduce_scatter | solution.py:82
  147.9 2.0 copy.83
  149.9 34.1 %all_to_all.11 = bf16[8,18,3,1024]{3,2,1,0:T(4,128)(2,1)S(1)} all-to-all(bf16[8,18,3,1024]{3,2,1,0:T(4,128)(2,1)S(1)} %copy.83), channel_id=1, replica_groups=mesh['dp'=8,'expert'=2,'tensor'=2] {'dp'}, dimensions={0} | all-to-all | bytes 1769472 | tf_op jit(solution)/shard_map/all_to_all | solution.py:85
  184.0 1.6 copy.84
  185.7 27.1 %all-gather.2.cloned.1.call-done = bf16[8,18,3,2048]{3,0,2,1:T(8,128)(2,1)} async-done(((bf16[8,18,3,1024]{3,0,2,1:T(8,128)(2,1)}), bf16[8,18,3,2048]{3,0,2,1:T(8,128)(2,1)}) %all-gather.2.cloned.1.call-update) | async-done | bytes 1769488 | tf_op jit(solution)/shard_map/all_gather | solution.py:90
  212.9 5.2 %copy.98 = f32[8,18,3,2048]{3,2,1,0:T(4,128)} copy(bf16[8,18,3,2048]{3,0,2,1:T(8,128)(2,1)} %all-gather.2.cloned.1.call-done) | data formatting | bytes 5308416 | tf_op jit(solution)/shard_map/reshape | solution.py:93
  218.1 7.1 %gather_fusion = f32[128,3,2048]{2,1,0:T(4,128)} fusion(f32[144,3,2048]{2,1,0:T(4,128)} %bitcast.139, s32[1024]{0:T(1024)S(1)} %pad_clamp_fusion), kind=kCustom, calls=%fused_computation | custom fusion | bytes 6291968 | tf_op jit(solution)/shard_map/gather | solution.py:93
  225.2 8.2 %fusion.43 = (f32[64,2,1,2048]{3,2,1,0:T(1,128)S(1)}, f32[64,2,1,2048]{3,2,1,0:T(1,128)S(1)}, f32[64,2,1,2048]{3,2,1,0:T(1,128)S(1)}) fusion(f32[64,2,3,2048]{3,2,1,0:T(4,128)} %bitcast.140), kind=kLoop, calls=%fused_computation.104 | loop fusion | bytes 6291456 | tf_op jit(solution)/shard_map/slice | solution.py:98
  233.4 2.3 fusion.23
  236.0 2.5 psum.43
  239.5 4.2 %multiply_reduce_fusion.1 = (f32[64,2]{1,0:T(8,128)S(1)}, f32[64,2]{1,0:T(8,128)S(1)}, f32[64,2]{1,0:T(8,128)S(1)}, f32[64,2]{1,0:T(8,128)S(1)}, f32[64,2]{1,0:T...) fusion(f32[64,2,1,2048]{3,2,1,0:T(1,128)S(1)} %get-tuple-element.32, f32[64,2048]{1,0:T(8,128)S(1)} %get-tuple-element.33, ...), kind=kLoop, calls=%fused_computation.37 | loop fusion | flops 4455552 | bytes 3682304 | tf_op jit(solution)/shard_map/reduce_sum | solution.py:119
  244.3 2.5 all-reduce.1
  247.6 21.4 %all-reduce = (f32[8]{0:T(128)S(1)}, f32[8]{0:T(128)S(1)}) all-reduce(f32[8]{0:T(128)S(1)} %get-tuple-element.18, f32[8]{0:T(128)S(1)} %get-tuple-element.17), channel_id=1, replica_groups=mesh['dp'=8,'expert'=2,'tensor'=2] {'dp'}, use_global_device_ids=true, to_apply=%region_20.21 | all-reduce | flops 16 | bytes 128 | tf_op jit(solution)/shard_map/psum | solution.py:137
  (60 shorter events, 9.7 us)
Async XLA Ops:
  7.2 80.0 %all-reduce.4.cloned.1.call-start = ((), (), s32[]{:S(2)}) async-start(), calls=%async_computation.3 | async-start | bytes 7077888 | tf_op jit(solution)/shard_map/psum | solution.py:76
  40.1 10.5 %copy-start = (bf16[2048,4096]{1,0:T(8,128)(2,1)S(1)}, bf16[2048,4096]{1,0:T(8,128)(2,1)}, u32[]{:S(2)}) copy-start(bf16[2048,4096]{1,0:T(8,128)(2,1)} %param.15) | copy-start | bytes 50331652
  63.9 84.0 %reduce-scatter.2.cloned.1.call-start = ((), (), s32[]{:S(2)}) async-start(), calls=%async_computation.4 | async-start | bytes 3538944 | tf_op jit(solution)/shard_map/reduce_scatter | solution.py:82
  111.7 101.1 %all-gather.2.cloned.1.call-start = ((), (), s32[]{:S(2)}) async-start(), calls=%async_computation.5 | async-start | bytes 2654208 | tf_op jit(solution)/shard_map/all_gather | solution.py:90
  149.9 35.7 %copy-start.5 = (f32[64,2]{0,1:T(2,128)S(1)}, f32[64,2]{0,1:T(2,128)}, u32[]{:S(2)}) copy-start(f32[64,2]{0,1:T(2,128)} %param.13) | copy-start | bytes 1540
  149.9 35.8 %copy-start.3 = (f32[2048]{0:T(1024)S(1)}, f32[2048]{0:T(1024)}, u32[]{:S(2)}) copy-start(f32[2048]{0:T(1024)} %param.11) | copy-start | bytes 24580
  225.2 10.5 %copy-start.1 = (bf16[64,2048]{1,0:T(8,128)(2,1)S(1)}, bf16[64,2048]{1,0:T(8,128)(2,1)}, u32[]{:S(2)}) copy-start(bf16[64,2048]{1,0:T(8,128)(2,1)} %param.9) | copy-start | bytes 786436
  233.4 5.1 %copy-start.2 = (bf16[64,2048]{1,0:T(8,128)(2,1)S(1)}, bf16[64,2048]{1,0:T(8,128)(2,1)}, u32[]{:S(2)}) copy-start(bf16[64,2048]{1,0:T(8,128)(2,1)} %param.10) | copy-start | bytes 786436
  239.5 7.9 %copy-start.4 = (s32[64,2]{0,1:T(2,128)S(1)}, s32[64,2]{0,1:T(2,128)}, u32[]{:S(2)}) copy-start(s32[64,2]{0,1:T(2,128)} %param.12) | copy-start | bytes 1540
Sparse Core Ops, SparseCore 0:
  64.0 23.1 all-reduce.3
  111.8 35.9 reduce-scatter.1
  185.7 27.0 all-gather.1
where the time goes:
time: 276 us
  blocking collectives  87.7 us (32%)
  waiting for transfers between devices  86.3 us (31%)
  matrix products  35.5 us (13%)
  local copies, waits for them, and re-layouts  34.8 us (13%)
  other arithmetic  17.4 us (6%)
  between operations  14 us (5%)
    reduce_scatter x1, waiting for transfers between devices, on_device(): lax.psum_scatter(images.astype(jnp.float32).astype(jnp.bfloat16), 'expert...  36.1 us
    all_to_all x1, blocking collectives, on_device(): lax.all_to_all(halves.astype(jnp.bfloat16), 'dp', split_axis=0, concat_ax...  34.1 us
    all_to_all x1, blocking collectives, on_device(): lax.all_to_all(outgoing, 'dp', split_axis=0, concat_axis=0, tiled=True)  27.3 us
    all_gather x1, waiting for transfers between devices, on_device(): lax.all_gather(grouped.astype(jnp.bfloat16), 'expert', axis=3, tiled=True)  27.1 us
    psum x1, waiting for transfers between devices, on_device(): lax.psum(partial_value.astype(jnp.bfloat16), 'tensor').astype(jnp.float32)  23 us
    psum x1, blocking collectives, on_device(): lax.psum((jnp.sum(member * curvature[:, :, None], axis=(0, 1)), jnp.sum(m...  21.4 us
    dot_general x1, matrix products, on_device(): jnp.dot(hidden_jets.reshape(-1, hidden_part), w_down, preferred_element_t...  15.9 us
    dot_general x1, matrix products, on_device(): jnp.dot(expert_rows, w_gate, preferred_element_type=jnp.float32)  8.53 us
  transfers between devices with their start and end apart: 3, of which 3 were waited for; matrix products, arithmetic and copies ran while one was open for 0% of the time, Pallas kernels for 0%

commit v1 on v0

v1 whole, which is shorter than its diff:
```python
import functools

import jax
import jax.numpy as jnp
from jax import lax
from jax.experimental import pallas as pl
from jax.experimental.pallas import tpu as pltpu
from jax.sharding import PartitionSpec as P


D = 4096
EXPERTS = 8
CAP = 18
LANE_PARTS = 4
OUT_ROWS = 56
GROUP = 4
PAIR = 2
PART_ROWS = 80
HIDDEN_CHUNKS = 4
MIB = 1024 * 1024

epsilon = 1e-05
loss_weight = 8.0
f32 = jnp.float32
bf16 = jnp.bfloat16


def in_hbm(array):
    return pltpu.with_memory_space_constraint(array, pltpu.HBM)


def in_vmem(array):
    return pltpu.with_memory_space_constraint(array, pltpu.VMEM)


def slot_rows(ids):
    count = ids.shape[1]
    line = lax.broadcasted_iota(jnp.int32, (EXPERTS, count), 0)
    rows = [ids[i : i + 1, :] for i in range(2)]
    hots = [(line == r).astype(f32) for r in rows]
    earlier = lax.broadcasted_iota(jnp.int32, (count, count), 0) < lax.broadcasted_iota(
        jnp.int32, (count, count), 1
    )
    before = jnp.dot(
        (hots[0] + hots[1]).astype(bf16), earlier.astype(bf16), preferred_element_type=f32
    )
    slots = [jnp.sum(before * h, axis=0, keepdims=True).astype(jnp.int32) for h in hots]
    return rows, hots, slots


def upright(row):
    count = row.shape[1]
    same = lax.broadcasted_iota(jnp.int32, (count, count), 0) == lax.broadcasted_iota(
        jnp.int32, (count, count), 1
    )
    return jnp.sum(jnp.where(same, row, jnp.zeros_like(row)), axis=1, keepdims=True)


def dispatch_body(where_ref, ids_ref, tokens_hbm, *refs):
    outs, (tokens_ref, sem) = refs[:EXPERTS], refs[EXPERTS:]
    fetch = pltpu.make_async_copy(tokens_hbm, tokens_ref, sem)
    fetch.start()
    rows, _, slots = slot_rows(ids_ref[...])
    block = LANE_PARTS * CAP
    line = lax.broadcasted_iota(jnp.int32, (EXPERTS * block, ids_ref.shape[1]), 0)
    firsts = [(r ^ where_ref[1]) * block + s for r, s in zip(rows, slots)]
    selects = []
    for q in range(LANE_PARTS):
        hit = [line == first + q * CAP for first in firsts]
        selects.append((hit[0] | hit[1]).astype(f32).astype(bf16))
    lanes = outs[0].shape[1]
    fetch.wait()
    out = None
    for q in range(LANE_PARTS):
        term = jnp.dot(
            selects[q], tokens_ref[:, q * lanes : (q + 1) * lanes], preferred_element_type=f32
        )
        out = term if out is None else out + term
    for j in range(EXPERTS):
        outs[j][...] = out[j * block : (j + 1) * block].astype(bf16)


def dispatch(where, ids_t, tokens):
    rows, width = tokens.shape
    vmem = pl.BlockSpec(memory_space=pltpu.VMEM)
    return pl.pallas_call(
        dispatch_body,
        out_shape=[jax.ShapeDtypeStruct((LANE_PARTS * CAP, width // LANE_PARTS), bf16)] * EXPERTS,
        in_specs=[pl.BlockSpec(memory_space=pltpu.SMEM), vmem, pl.BlockSpec(memory_space=pltpu.HBM)],
        out_specs=[vmem] * EXPERTS,
        scratch_shapes=[pltpu.VMEM((rows, width), bf16), pltpu.SemaphoreType.DMA],
        compiler_params=pltpu.CompilerParams(vmem_limit_bytes=8 * MIB),
        name="dispatch",
    )(where, ids_t, in_hbm(tokens))


def fetch_body(*refs):
    count = (len(refs) - 1) // 2
    sems = refs[-1]
    copies = [
        pltpu.make_async_copy(refs[i], refs[count + i], sems.at[i]) for i in range(count)
    ]
    for copy in copies:
        copy.start()
    for copy in copies:
        copy.wait()


def fetch(*arrays):
    return pl.pallas_call(
        fetch_body,
        out_shape=[pltpu.VMEM(a.shape, a.dtype) for a in arrays],
        in_specs=[pl.BlockSpec(memory_space=pltpu.HBM)] * len(arrays),
        out_specs=[pl.BlockSpec(memory_space=pltpu.VMEM)] * len(arrays),
        scratch_shapes=[pltpu.SemaphoreType.DMA((len(arrays),))],
        compiler_params=pltpu.CompilerParams(vmem_limit_bytes=MIB),
        cost_estimate=pl.CostEstimate(
            flops=3 * 10**9 * len(arrays), bytes_accessed=sum(2 * a.size for a in arrays), transcendentals=0
        ),
        name="fetch",
    )(*[in_hbm(a) for a in arrays])


def preact_body(first, count, *refs):
    blocks = refs[:count]
    near_ref, *far, out_ref, rows_ref, held_ref, sems = refs[count:]
    size = out_ref.shape[2]
    steps = sems.shape[1]
    tile = size // steps
    copies = [
        [
            pltpu.make_async_copy(
                hbm.at[:, pl.ds(first + t * tile, tile)],
                held_ref.at[w, :, pl.ds(t * tile, tile)],
                sems.at[w, t],
            )
            for t in range(steps)
        ]
        for w, hbm in enumerate(far)
    ]
    for copy in sum(copies, []):
        copy.start()
    lanes = blocks[0].shape[1]
    tail = jnp.zeros((PART_ROWS - GROUP * CAP, lanes), f32)
    for g in range(count // GROUP):
        mine = [blocks[g * GROUP + i][...].astype(f32) for i in range(GROUP)]
        for q in range(LANE_PARTS):
            rows_ref[g * PART_ROWS : (g + 1) * PART_ROWS, q * lanes : (q + 1) * lanes] = (
                jnp.concatenate([b[q * CAP : (q + 1) * CAP] for b in mine] + [tail], axis=0)
            ).astype(bf16)
    rows = rows_ref[...]
    for part in range(3):
        for t in range(steps):
            if part:
                copies[part - 1][t].wait()
                weight = held_ref[part - 1, :, t * tile : (t + 1) * tile]
            else:
                weight = near_ref[:, first + t * tile : first + (t + 1) * tile]
            out_ref[part, :, t * tile : (t + 1) * tile] = jnp.dot(
                rows, weight, preferred_element_type=f32
            ).astype(bf16)


def preact(arrived, near, far, chunk, size):
    count = len(arrived)
    width = near.shape[0]
    total = count // GROUP * PART_ROWS
    vmem = pl.BlockSpec(memory_space=pltpu.VMEM)
    steps = max(1, size // 256)
    return pl.pallas_call(
        functools.partial(preact_body, chunk * size, count),
        out_shape=jax.ShapeDtypeStruct((3, total, size), bf16),
        in_specs=[vmem] * (count + 1) + [pl.BlockSpec(memory_space=pltpu.HBM)] * 2,
        out_specs=vmem,
        scratch_shapes=[
            pltpu.VMEM((total, width), bf16),
            pltpu.VMEM((2, width, size), bf16),
            pltpu.SemaphoreType.DMA((2, steps)),
        ],
        compiler_params=pltpu.CompilerParams(vmem_limit_bytes=16 * MIB),
        cost_estimate=pl.CostEstimate(
            flops=6 * total * width * size, bytes_accessed=6 * width * size, transcendentals=0
        ),
        name="preact",
    )(*arrived, in_vmem(near), *[in_hbm(w) for w in far])


def jets_body(first, own_ref, peer_ref, down_hbm, *refs):
    outs = refs[:-2]
    down_ref, sem = refs[-2:]
    copy = pltpu.make_async_copy(down_hbm.at[pl.ds(first, down_ref.shape[0])], down_ref, sem)
    copy.start()
    size = own_ref.shape[2]
    tile = min(512, size)
    for g, out in enumerate(outs):

        @pl.loop(0, PART_ROWS // 16)
        def _(step):
            at = pl.multiple_of(step * 16, 16)
            for t in range(size // tile):
                lane = pl.ds(t * tile, tile)
                place = (pl.ds(g * PART_ROWS + at, 16), lane)
                gate_in, gate_dir, up_in = (
                    own_ref[(i,) + place].astype(f32) + peer_ref[(i,) + place].astype(f32)
                    for i in range(3)
                )
                turn = jnp.tanh(0.5 * gate_in)
                sig = 0.5 + 0.5 * turn
                rest = 0.5 - 0.5 * turn
                first_slope = sig * (1.0 + gate_in * rest)
                second_slope = (sig * rest) * (2.0 - gate_in * turn)
                along = gate_dir * up_in
                parts = (
                    (gate_in * sig) * up_in,
                    first_slope * along,
                    second_slope * (gate_dir * along),
                )
                for i, part in enumerate(parts):
                    out[i, pl.ds(at, 16), lane] = part.astype(bf16)

    copy.wait()


def jets(own, peer, w_down, chunk, groups):
    _, rows, size = own.shape
    vmem = pl.BlockSpec(memory_space=pltpu.VMEM)
    return pl.pallas_call(
        functools.partial(jets_body, chunk * size),
        out_shape=[jax.ShapeDtypeStruct((3, PART_ROWS, size), bf16)] * groups
        + [pltpu.VMEM((size, w_down.shape[1]), bf16)],
        in_specs=[vmem, vmem, pl.BlockSpec(memory_space=pltpu.HBM)],
        out_specs=[vmem] * (groups + 1),
        scratch_shapes=[pltpu.SemaphoreType.DMA],
        compiler_params=pltpu.CompilerParams(vmem_limit_bytes=8 * MIB),
        cost_estimate=pl.CostEstimate(
            flops=40 * 3 * rows * size, bytes_accessed=18 * rows * size, transcendentals=rows * size
        ),
        name="jets",
    )(own, peer, in_hbm(w_down))


def images_body(chunks, other, where_ref, *refs):
    hidden = refs[:chunks]
    down = refs[chunks : 2 * chunks]
    outs = refs[2 * chunks :]
    size = hidden[0].shape[2]
    width = outs[0].shape[2]
    tile = min(256, width)
    half = 1 - where_ref[0] if other else where_ref[0]
    for t in range(width // tile):
        lanes = pl.ds(pl.multiple_of(half * width + t * tile, tile), tile)
        acc = None
        for c in range(chunks):
            left = hidden[c][...].reshape(3 * PART_ROWS, size)
            term = jnp.dot(left, down[c][:, lanes], preferred_element_type=f32)
            acc = term if acc is None else acc + term
        tail = jnp.zeros((OUT_ROWS - 3 * CAP, tile), f32)
        for i in range(GROUP):
            first = [p * PART_ROWS + i * CAP for p in range(3)]
            outs[i // PAIR][i % PAIR, :, t * tile : (t + 1) * tile] = jnp.concatenate(
                [acc[r : r + CAP] for r in first] + [tail], axis=0
            ).astype(bf16)


def images(where, other, hidden, down):
    chunks = len(hidden)
    size = hidden[0].shape[2]
    width = down[0].shape[1] // 2
    vmem = pl.BlockSpec(memory_space=pltpu.VMEM)
    return pl.pallas_call(
        functools.partial(images_body, chunks, other),
        in_specs=[pl.BlockSpec(memory_space=pltpu.SMEM)] + [vmem] * (2 * chunks),
        out_specs=[vmem] * (GROUP // PAIR),
        out_shape=[jax.ShapeDtypeStruct((PAIR, OUT_ROWS, width), bf16)] * (GROUP // PAIR),
        compiler_params=pltpu.CompilerParams(vmem_limit_bytes=8 * MIB),
        cost_estimate=pl.CostEstimate(
            flops=6 * GROUP * CAP * chunks * size * width,
            bytes_accessed=2 * chunks * size * width,
            transcendentals=0,
        ),
        name="images",
    )(where, *hidden, *[in_vmem(d) for d in down])


def moments_body(count, where_ref, ids_ref, prob_ref, tokens_ref, targets_ref, gain_ref, *refs):
    blocks = refs[:count]
    stats_ref, summed_ref, sent_ref = refs[count:]
    holders = count // EXPERTS
    mine = where_ref[1]
    ids, _, slots = slot_rows(ids_ref[...])
    rows = ids[0].shape[1]
    starts = [upright((r ^ mine) * (holders * OUT_ROWS) + s) for r, s in zip(ids, slots)]
    table = jnp.concatenate([b[...].astype(f32) for b in blocks], axis=0).astype(bf16)
    lanes = lax.broadcasted_iota(jnp.int32, (rows, count * OUT_ROWS), 1)
    pieces = []
    for part in range(3):
        for i in range(2):
            hit = None
            for j in range(holders):
                same = lanes == starts[i] + (j * OUT_ROWS + part * CAP)
                hit = same if hit is None else hit | same
            pieces.append(hit.astype(f32))
    select = jnp.concatenate(pieces, axis=0).astype(bf16)
    picked = jnp.dot(select, table, preferred_element_type=f32)
    probs = [upright(prob_ref[i : i + 1, :]) for i in range(2)]
    part_of = lambda part, i: picked[(2 * part + i) * rows : (2 * part + i + 1) * rows] * probs[i]
    summed = tokens_ref[...].astype(f32) + (part_of(0, 0) + part_of(0, 1))
    summed_ref[...] = summed
    gain = gain_ref[...]
    sent_ref[...] = (gain * summed).astype(bf16)
    weighted = gain * gain * summed
    aim = gain * targets_ref[...].astype(f32)
    total = lambda v: jnp.sum(v, axis=1, keepdims=True)
    columns = [total(summed * summed), total(weighted * summed), total(aim * summed)]
    for i in range(2):
        along, bend = part_of(1, i), part_of(2, i)
        columns += [
            total(summed * along),
            total(along * along),
            total(summed * bend),
            total(gain * gain * along * along),
            total(weighted * along),
            total(weighted * bend),
            total(aim * along),
            total(aim * bend),
        ]
    place = lax.broadcasted_iota(jnp.int32, (rows, 128), 1)
    stats = jnp.zeros((rows, 128), f32)
    for c, column in enumerate(columns):
        stats = jnp.where(place == c, column, stats)
    stats_ref[...] = stats


def moments(where, ids_t, prob_t, tokens, targets, gain, blocks):
    count = len(blocks)
    rows = tokens.shape[0]
    half = tokens.shape[1] // 2
    whole = lambda shape: pl.BlockSpec(shape, lambda i, w: (0,) * len(shape))
    split = lambda r: pl.BlockSpec((r, half), lambda i, w: (0, w[0]))
    return pl.pallas_call(
        functools.partial(moments_body, count),
        grid_spec=pltpu.PrefetchScalarGridSpec(
            num_scalar_prefetch=1,
            grid=(1,),
            in_specs=[whole((2, rows)), whole((2, rows)), split(rows), split(rows), split(1)]
            + [whole((OUT_ROWS, half))] * count,
            out_specs=[whole((rows, 128)), whole((rows, half)), whole((rows, half))],
        ),
        out_shape=[
            jax.ShapeDtypeStruct((rows, 128), f32),
            jax.ShapeDtypeStruct((rows, half), f32),
            jax.ShapeDtypeStruct((rows, half), bf16),
        ],
        compiler_params=pltpu.CompilerParams(vmem_limit_bytes=40 * MIB),
        cost_estimate=pl.CostEstimate(
            flops=12 * rows * count * OUT_ROWS * half, bytes_accessed=MIB, transcendentals=0
        ),
        name="moments",
    )(where, ids_t, prob_t, tokens, targets, gain, *blocks)


def curve_body(
    where_ref, ids_ref, stats_ref, more_ref, summed_ref, gain_ref, other_ref, *outs
):
    normed_ref, curve_ref, sums_ref = outs
    stats = stats_ref[...] + more_ref[...]
    rows = stats.shape[0]
    col = lambda c: stats[:, c : c + 1]
    inv_root = lax.rsqrt(col(0) / D + epsilon)
    side = where_ref[0]
    width = summed_ref.shape[1]
    near = pl.ds(pl.multiple_of(side * width, width), width)
    far = pl.ds(pl.multiple_of((1 - side) * width, width), width)
    normed_ref[:, near] = (gain_ref[...] * summed_ref[...] * inv_root).astype(bf16)
    normed_ref[:, far] = (other_ref[...].astype(f32) * inv_root).astype(bf16)
    weighted_uu = col(1)
    resid_u = inv_root * weighted_uu - col(2)
    inv_cube = inv_root * inv_root * inv_root
    lanes = lax.broadcasted_iota(jnp.int32, (rows, 128), 1)
    totals = jnp.zeros((rows, 128), f32)
    counts = jnp.zeros((rows, 128), f32)
    for i in range(2):
        ua, aa, ub, waa, wau, wub, ta, tb = (col(3 + 8 * i + j) for j in range(8))
        resid_a = inv_root * wau - ta
        resid_b = inv_root * wub - tb
        first_rate = 2.0 * ua / D
        second_rate = 2.0 * (aa + ub) / D
        slope_one = -0.5 * inv_cube * first_rate
        slope_two = (
            0.75 * inv_cube * inv_root * inv_root * first_rate * first_rate
            - 0.5 * inv_cube * second_rate
        )
        tangent_sq = (
            inv_root * inv_root * waa
            + 2.0 * inv_root * slope_one * wau
            + slope_one * slope_one * weighted_uu
        )
        bending = inv_root * resid_b + 2.0 * slope_one * resid_a + slope_two * resid_u
        curvature = 2.0 * loss_weight / D * (tangent_sq + bending)
        curve_ref[:, i : i + 1] = curvature
        member = (lanes == upright(ids_ref[i : i + 1, :])).astype(f32)
        totals = totals + member * curvature
        counts = counts + member
    line = lax.broadcasted_iota(jnp.int32, (8, 128), 0)
    sums_ref[...] = jnp.where(
        line == 0,
        jnp.sum(totals, axis=0, keepdims=True),
        jnp.where(line == 1, jnp.sum(counts, axis=0, keepdims=True), 0.0),
    )


def curve(where, ids_t, stats, more, summed, gain, other):
    rows, half = summed.shape
    whole = lambda shape: pl.BlockSpec(shape, lambda i, w: (0,) * len(shape))
    return pl.pallas_call(
        curve_body,
        grid_spec=pltpu.PrefetchScalarGridSpec(
            num_scalar_prefetch=1,
            grid=(1,),
            in_specs=[
                whole((2, rows)),
                whole((rows, 128)),
                whole((rows, 128)),
                whole((rows, half)),
                pl.BlockSpec((1, half), lambda i, w: (0, w[0])),
                whole((rows, half)),
            ],
            out_specs=[whole((rows, 2 * half)), whole((rows, 2)), whole((8, 128))],
        ),
        out_shape=[
            jax.ShapeDtypeStruct((rows, 2 * half), bf16),
            jax.ShapeDtypeStruct((rows, 2), f32),
            jax.ShapeDtypeStruct((8, 128), f32),
        ],
        compiler_params=pltpu.CompilerParams(vmem_limit_bytes=12 * MIB),
        name="curve",
    )(where, ids_t, stats, more, summed, gain, other)


def swap(value, axis, mask=1):
    n = lax.axis_size(axis)
    return lax.ppermute(value, axis, [(i, i ^ mask) for i in range(n)])


def layer(tokens, targets, norm_gain, expert_ids, gate_prob, w_gate, gate_probe, w_up, w_down):
    n = lax.axis_size("dp")
    holders = n // EXPERTS
    hidden_part = w_gate.shape[1]
    where = jnp.stack([lax.axis_index("expert"), lax.axis_index("dp") // holders]).astype(jnp.int32)
    gain = norm_gain.reshape(1, -1)
    ids_t, prob_t = expert_ids.T, gate_prob.T

    outgoing = dispatch(where, ids_t, tokens)
    arrived = [outgoing[0]] * n
    for k in range(1, n):
        arrived[k] = swap(outgoing[k // holders], "dp", k)
    (near_gate,) = fetch(w_gate)

    size = hidden_part // HIDDEN_CHUNKS
    groups = n // GROUP
    hidden = [[] for _ in range(groups)]
    down = []
    for c in range(HIDDEN_CHUNKS):
        own = preact(arrived, near_gate, (gate_probe, w_up), c, size)
        *parts, rows = jets(own, swap(own, "tensor"), w_down, c, groups)
        down.append(rows)
        for g, part in enumerate(parts):
            hidden[g].append(part)

    returned = [None] * n
    for g in range(groups - 1, -1, -1):
        theirs = images(where, True, hidden[g], down)
        got = [swap(v, "expert") for v in theirs]
        ours = images(where, False, hidden[g], down)
        for i in range(GROUP - 1, -1, -1):
            k = g * GROUP + i
            pair = [v[i // PAIR][i % PAIR].astype(f32) for v in (ours, got)]
            both = (pair[0] + pair[1]).astype(bf16)
            returned[k] = swap(both, "dp", k) if k else both

    stats, summed, sent = moments(where, ids_t, prob_t, tokens, targets, gain, returned)
    other = swap(sent, "expert")
    stats = stats + swap(stats, "tensor")
    more = swap(stats, "expert")
    normed, curvature, sums = curve(where, ids_t, stats, more, summed, gain, other)
    step = n // 2
    while step:
        sums = sums + swap(sums, "dp", step)
        step //= 2
    return (normed, curvature, sums[0, :EXPERTS] / sums[1, :EXPERTS])


def solution(mesh):
    return jax.shard_map(
        layer,
        mesh=mesh,
        in_specs=(
            P("dp", "tensor"),
            P("dp", "tensor"),
            P("tensor"),
            P("dp", None),
            P("dp", None),
            P("tensor", ("dp", "expert")),
            P("tensor", ("dp", "expert")),
            P("tensor", ("dp", "expert")),
            P(("dp", "expert"), "tensor"),
        ),
        out_specs=(P("dp", "tensor"), P("dp", None), P()),
        check_vma=False,
    )
```

time: 276 us -> 126 us (0.46)
  blocking collectives: 87.7 us -> 0 us
  waiting for transfers between devices: 86.3 us -> 22.2 us
  Pallas kernels: 0 us -> 55.3 us
  starting transfers between devices: 0.3 us -> 44.8 us
  matrix products: 35.5 us -> 0 us
  local copies, waits for them, and re-layouts: 34.8 us -> 1.34 us
  other arithmetic: 17.4 us -> 0.84 us
  between operations: 14 us -> 0.92 us
    all_to_all x2 -> x0, blocking collectives: 61.3 us -> none  [the longest x1 34.1 us: on_device(): lax.all_to_all(halves.astype(jnp.bfloat16), 'dp', split_axis=0, concat_ax...]
    pallas_call x0 -> x16, Pallas kernels: none -> 55.3 us  [the longest x4 23.9 us: preact(): pl.pallas_call(functools.partial(preact_body, chunk * size, count), out_s...]
    ppermute x0 -> x28, starting transfers between devices: none -> 44.8 us  [swap(): return lax.ppermute(value, axis, [(i, i ^ mask) for i in range(n)])]
    reduce_scatter x1 -> x0, waiting for transfers between devices: 36.1 us -> none  [on_device(): lax.psum_scatter(images.astype(jnp.float32).astype(jnp.bfloat16), 'expert...]
    dot_general x4 -> x0, matrix products: 35.5 us -> none  [the longest x1 15.9 us: on_device(): jnp.dot(hidden_jets.reshape(-1, hidden_part), w_down, preferred_element_t...]
    all_gather x1 -> x0, waiting for transfers between devices: 27.1 us -> none  [on_device(): lax.all_gather(grouped.astype(jnp.bfloat16), 'expert', axis=3, tiled=True)]
    psum x3 -> x0, blocking collectives: 26.3 us -> none  [the longest x1 21.4 us: on_device(): lax.psum((jnp.sum(member * curvature[:, :, None], axis=(0, 1)), jnp.sum(m...]
    psum x1 -> x0, waiting for transfers between devices: 23 us -> none  [on_device(): lax.psum(partial_value.astype(jnp.bfloat16), 'tensor').astype(jnp.float32)]
  transfers between devices with their start and end apart: 3 -> 28, of which waited for: 3 -> 9; matrix products, arithmetic and copies ran while one was open for 0% -> 1% of each run, Pallas kernels for 0% -> 29%
where the time goes in v1:
time: 126 us; the launch traced here: 125 us
  Pallas kernels  55.3 us (44%)
  starting transfers between devices  44.8 us (36%)
  waiting for transfers between devices  22.2 us (18%)
  local copies, waits for them, and re-layouts  1.34 us (1%)
    ppermute x28, starting transfers between devices, swap(): return lax.ppermute(value, axis, [(i, i ^ mask) for i in range(n)])  44.8 us
    pallas_call x4, Pallas kernels, preact(): pl.pallas_call(functools.partial(preact_body, chunk * size, count), out_s...  23.9 us
    ppermute x28, waiting for transfers between devices, swap(): return lax.ppermute(value, axis, [(i, i ^ mask) for i in range(n)])  22.2 us
    pallas_call x4, Pallas kernels, images(): pl.pallas_call(functools.partial(images_body, chunks, other), in_specs=[p...  11.3 us
    pallas_call x4, Pallas kernels, jets(): pl.pallas_call(functools.partial(jets_body, chunk * size), out_shape=[jax...  8.8 us
    pallas_call x1, Pallas kernels, fetch(): pl.pallas_call(fetch_body, out_shape=[pltpu.VMEM(a.shape, a.dtype) for a...  5.78 us
  transfers between devices with their start and end apart: 28, of which 9 were waited for; matrix products, arithmetic and copies ran while one was open for 1% of the time, Pallas kernels for 29%

profile of v1, /device:TPU:0, one launch (start us, length us, event | category | flops | bytes accessed | tf_op | source)
XLA Modules:
  0.0 125.4 jit_solution(2733536029208670787)
XLA Ops:
  1.4 2.2 %dispatch.1 = (bf16[72,512]{1,0:T(8,128)(2,1)S(1)}, bf16[72,512]{1,0:T(8,128)(2,1)S(1)}, bf16[72,512]{1,0:T(8,128)(2,1)S(1)}, bf16[72,512]{1,0:T(8,128)(2,1)S(1)...) custom-call(s32[2]{0:T(128)S(1)} %pad_add_fusion.where_ref, ...), custom_call_target="tpu_custom_call" | custom-call | tf_op jit(solution)/shard_map/dispatch/pallas_call | solution.py:86
  3.6 3.1 %collective-permute-start = (bf16[72,512]{1,0:T(8,128)(2,1)S(1)}, bf16[72,512]{1,0:T(8,128)(2,1)S(1)}, u32[]{:S(2)}, u32[]{:S(2)}) collective-permute-start(bf16[72,512]{1,0:T(8,128)(2,1)S(1)} %get-tuple-element.38), channel_id=1, source_target_pairs={{0,4},{4,0},{8,12},{12,8},{16,20},{20,16},{24,28},{28,24},{1,5},{5... | collective-permute-start | bytes 221192 | tf_op jit(solution)/shard_map/ppermute | solution.py:442
  8.3 3.0 %collective-permute-start.3 = (bf16[72,512]{1,0:T(8,128)(2,1)S(1)}, bf16[72,512]{1,0:T(8,128)(2,1)S(1)}, u32[]{:S(2)}, u32[]{:S(2)}) collective-permute-start(bf16[72,512]{1,0:T(8,128)(2,1)S(1)} %get-tuple-element.41), channel_id=1, source_target_pairs={{0,16},{4,20},{8,24},{12,28},{16,0},{20,4},{24,8},{28,12},{1,17},{... | collective-permute-start | bytes 221192 | tf_op jit(solution)/shard_map/ppermute | solution.py:442
  12.6 3.6 %collective-permute-start.5 = (bf16[72,512]{1,0:T(8,128)(2,1)S(1)}, bf16[72,512]{1,0:T(8,128)(2,1)S(1)}, u32[]{:S(2)}, u32[]{:S(2)}) collective-permute-start(bf16[72,512]{1,0:T(8,128)(2,1)S(1)} %get-tuple-element.43), channel_id=1, source_target_pairs={{0,24},{4,28},{8,16},{12,20},{16,8},{20,12},{24,0},{28,4},{1,25},{... | collective-permute-start | bytes 221192 | tf_op jit(solution)/shard_map/ppermute | solution.py:442
  16.2 5.8 %fetch.1.refs_8_ = bf16[2048,4096]{1,0:T(8,128)(2,1)S(1)} custom-call(bf16[2048,4096]{1,0:T(8,128)(2,1)} %refs_0_.1), custom_call_target="tpu_custom_call" | custom-call | flops 3000000000 | bytes 16777216 | tf_op jit(solution)/shard_map/fetch/pallas_call | solution.py:110
  23.3 5.9 %preact.5.own_ref = bf16[3,160,1024]{2,1,0:T(8,128)(2,1)S(1)} custom-call(bf16[72,512]{1,0:T(8,128)(2,1)S(1)} %get-tuple-element.37.refs_0_, bf16[72,512]{1,0:T(8,128)(2,1)S(1)} %collective-permute-done.refs_1_, bf16[72,512]{1,0:T(8,128)(2,1)S(1)} %collective-permute-done.1.refs_2_, bf16[72,512]{1,0:T(8,128)(2,1)S(1)} %collective-permute-done.2.refs_3_, ...), custom_call_target="tpu_custom_call" | custom-call | flops 2013265920 | bytes 12582912 | tf_op jit(solution)/shard_map/preact/pallas_call | solution.py:170
  29.3 5.9 %preact.6.own_ref = bf16[3,160,1024]{2,1,0:T(8,128)(2,1)S(1)} custom-call(bf16[72,512]{1,0:T(8,128)(2,1)S(1)} %get-tuple-element.37.refs_0_, bf16[72,512]{1,0:T(8,128)(2,1)S(1)} %collective-permute-done.refs_1_, bf16[72,512]{1,0:T(8,128)(2,1)S(1)} %collective-permute-done.1.refs_2_, bf16[72,512]{1,0:T(8,128)(2,1)S(1)} %collective-permute-done.2.refs_3_, ...), custom_call_target="tpu_custom_call" | custom-call | flops 2013265920 | bytes 12582912 | tf_op jit(solution)/shard_map/preact/pallas_call | solution.py:170
  35.8 5.9 %preact.7.own_ref = bf16[3,160,1024]{2,1,0:T(8,128)(2,1)S(1)} custom-call(bf16[72,512]{1,0:T(8,128)(2,1)S(1)} %get-tuple-element.37.refs_0_, bf16[72,512]{1,0:T(8,128)(2,1)S(1)} %collective-permute-done.refs_1_, bf16[72,512]{1,0:T(8,128)(2,1)S(1)} %collective-permute-done.1.refs_2_, bf16[72,512]{1,0:T(8,128)(2,1)S(1)} %collective-permute-done.2.refs_3_, ...), custom_call_target="tpu_custom_call" | custom-call | flops 2013265920 | bytes 12582912 | tf_op jit(solution)/shard_map/preact/pallas_call | solution.py:170
  41.8 6.1 %preact.4.own_ref = bf16[3,160,1024]{2,1,0:T(8,128)(2,1)S(1)} custom-call(bf16[72,512]{1,0:T(8,128)(2,1)S(1)} %get-tuple-element.37.refs_0_, bf16[72,512]{1,0:T(8,128)(2,1)S(1)} %collective-permute-done.refs_1_, bf16[72,512]{1,0:T(8,128)(2,1)S(1)} %collective-permute-done.1.refs_2_, bf16[72,512]{1,0:T(8,128)(2,1)S(1)} %collective-permute-done.2.refs_3_, ...), custom_call_target="tpu_custom_call" | custom-call | flops 2013265920 | bytes 12582912 | tf_op jit(solution)/shard_map/preact/pallas_call | solution.py:170
  50.7 2.2 %jets.6 = (bf16[3,80,1024]{2,1,0:T(8,128)(2,1)S(1)}, bf16[3,80,1024]{2,1,0:T(8,128)(2,1)S(1)}, bf16[1024,2048]{1,0:T(8,128)(2,1)S(1)}) custom-call(bf16[3,160,1024]{2,1,0:T(8,128)(2,1)S(1)} %preact.6.own_ref, bf16[3,160,1024]{2,1,0:T(8,128)(2,1)S(1)} %collective-permute-done.9.peer_ref, bf16[4096,2048]{1,0:T(8,128)(2,1)} %down_hbm.7), custom_call_target="tpu_custom_call" | custom-call | flops 19660800 | bytes 2949120 | tf_op jit(solution)/shard_map/jets/pallas_call | solution.py:227
  53.0 2.2 %jets.5 = (bf16[3,80,1024]{2,1,0:T(8,128)(2,1)S(1)}, bf16[3,80,1024]{2,1,0:T(8,128)(2,1)S(1)}, bf16[1024,2048]{1,0:T(8,128)(2,1)S(1)}) custom-call(bf16[3,160,1024]{2,1,0:T(8,128)(2,1)S(1)} %preact.5.own_ref, bf16[3,160,1024]{2,1,0:T(8,128)(2,1)S(1)} %collective-permute-done.8.peer_ref, bf16[4096,2048]{1,0:T(8,128)(2,1)} %down_hbm.7), custom_call_target="tpu_custom_call" | custom-call | flops 19660800 | bytes 2949120 | tf_op jit(solution)/shard_map/jets/pallas_call | solution.py:227
  57.4 2.8 %images.5 = (bf16[2,56,1024]{2,1,0:T(8,128)(2,1)S(1)}, bf16[2,56,1024]{2,1,0:T(8,128)(2,1)S(1)}) custom-call(s32[2]{0:T(128)S(1)} %pad_add_fusion.where_ref, bf16[3,80,1024]{2,1,0:T(8,128)(2,1)S(1)} %get-tuple-element.45.refs_0_, bf16[3,80,1024]{2,1,0:T(8,128)(2,1)S(1)} %get-tuple-element.46.refs_1_, bf16[3,80,1024]{2,1,0:T(8,128)(2,1)S(1)} %get-tuple-element.47.refs_2_, ...), custom_call_target="tpu_custom_call" | custom-call | flops 1811939328 | bytes 8388608 | tf_op jit(solution)/shard_map/images/pallas_call | solution.py:270
  60.2 2.8 %images.4 = (bf16[2,56,1024]{2,1,0:T(8,128)(2,1)S(1)}, bf16[2,56,1024]{2,1,0:T(8,128)(2,1)S(1)}) custom-call(s32[2]{0:T(128)S(1)} %pad_add_fusion.where_ref, bf16[3,80,1024]{2,1,0:T(8,128)(2,1)S(1)} %get-tuple-element.45.refs_0_, bf16[3,80,1024]{2,1,0:T(8,128)(2,1)S(1)} %get-tuple-element.46.refs_1_, bf16[3,80,1024]{2,1,0:T(8,128)(2,1)S(1)} %get-tuple-element.47.refs_2_, ...), custom_call_target="tpu_custom_call" | custom-call | flops 1811939328 | bytes 8388608 | tf_op jit(solution)/shard_map/images/pallas_call | solution.py:270
  65.2 2.8 %images.7 = (bf16[2,56,1024]{2,1,0:T(8,128)(2,1)S(1)}, bf16[2,56,1024]{2,1,0:T(8,128)(2,1)S(1)}) custom-call(s32[2]{0:T(128)S(1)} %pad_add_fusion.where_ref, bf16[3,80,1024]{2,1,0:T(8,128)(2,1)S(1)} %get-tuple-element.57.refs_0_, bf16[3,80,1024]{2,1,0:T(8,128)(2,1)S(1)} %get-tuple-element.58.refs_1_, bf16[3,80,1024]{2,1,0:T(8,128)(2,1)S(1)} %get-tuple-element.59.refs_2_, ...), custom_call_target="tpu_custom_call" | custom-call | flops 1811939328 | bytes 8388608 | tf_op jit(solution)/shard_map/images/pallas_call | solution.py:270
  70.1 2.8 %images.6 = (bf16[2,56,1024]{2,1,0:T(8,128)(2,1)S(1)}, bf16[2,56,1024]{2,1,0:T(8,128)(2,1)S(1)}) custom-call(s32[2]{0:T(128)S(1)} %pad_add_fusion.where_ref, bf16[3,80,1024]{2,1,0:T(8,128)(2,1)S(1)} %get-tuple-element.57.refs_0_, bf16[3,80,1024]{2,1,0:T(8,128)(2,1)S(1)} %get-tuple-element.58.refs_1_, bf16[3,80,1024]{2,1,0:T(8,128)(2,1)S(1)} %get-tuple-element.59.refs_2_, ...), custom_call_target="tpu_custom_call" | custom-call | flops 1811939328 | bytes 8388608 | tf_op jit(solution)/shard_map/images/pallas_call | solution.py:270
  73.7 2.8 %collective-permute-done.13 = bf16[2,56,1024]{2,1,0:T(8,128)(2,1)S(1)} collective-permute-done((bf16[2,56,1024]{2,1,0:T(8,128)(2,1)S(1)}, bf16[2,56,1024]{2,1,0:T(8,128)(2,1)S(1)}, u32[]{:S(2)}, u32[]{:S(2)}) %collective-permute-start.13) | collective-permute-done | bytes 229408 | tf_op jit(solution)/shard_map/ppermute | solution.py:442
  76.6 3.3 %collective-permute-start.15 = (bf16[56,1024]{1,0:T(8,128)(2,1)S(1)}, bf16[56,1024]{1,0:T(8,128)(2,1)S(1)}, u32[]{:S(2)}, u32[]{:S(2)}) collective-permute-start(bf16[56,1024]{1,0:T(8,128)(2,1)S(1)} %get-tuple-element.78), channel_id=1, source_target_pairs={{0,12},{4,8},{8,4},{12,0},{16,28},{20,24},{24,20},{28,16},{1,13},{... | collective-permute-start | bytes 344072 | tf_op jit(solution)/shard_map/ppermute | solution.py:442
  81.5 4.1 %collective-permute-start.18 = (bf16[56,1024]{1,0:T(8,128)(2,1)S(1)}, bf16[56,1024]{1,0:T(8,128)(2,1)S(1)}, u32[]{:S(2)}, u32[]{:S(2)}) collective-permute-start(bf16[56,1024]{1,0:T(8,128)(2,1)S(1)} %get-tuple-element.76), channel_id=1, source_target_pairs={{0,20},{4,16},{8,28},{12,24},{16,4},{20,0},{24,12},{28,8},{1,21},{... | collective-permute-start | bytes 344072 | tf_op jit(solution)/shard_map/ppermute | solution.py:442
  85.6 3.9 %collective-permute-start.17 = (bf16[56,1024]{1,0:T(8,128)(2,1)S(1)}, bf16[56,1024]{1,0:T(8,128)(2,1)S(1)}, u32[]{:S(2)}, u32[]{:S(2)}) collective-permute-start(bf16[56,1024]{1,0:T(8,128)(2,1)S(1)} %get-tuple-element.77), channel_id=1, source_target_pairs={{0,16},{4,20},{8,24},{12,28},{16,0},{20,4},{24,8},{28,12},{1,17},{... | collective-permute-start | bytes 344072 | tf_op jit(solution)/shard_map/ppermute | solution.py:442
  91.1 2.3 %collective-permute-start.20 = (bf16[56,1024]{1,0:T(8,128)(2,1)S(1)}, bf16[56,1024]{1,0:T(8,128)(2,1)S(1)}, u32[]{:S(2)}, u32[]{:S(2)}) collective-permute-start(bf16[56,1024]{1,0:T(8,128)(2,1)S(1)} %get-tuple-element.75), channel_id=1, source_target_pairs={{0,24},{4,28},{8,16},{12,20},{16,8},{20,12},{24,0},{28,4},{1,25},{... | collective-permute-start | bytes 344072 | tf_op jit(solution)/shard_map/ppermute | solution.py:442
  93.4 7.0 %collective-permute-done.17.refs_4_ = bf16[56,1024]{1,0:T(8,128)(2,1)S(1)} collective-permute-done((bf16[56,1024]{1,0:T(8,128)(2,1)S(1)}, bf16[56,1024]{1,0:T(8,128)(2,1)S(1)}, u32[]{:S(2)}, u32[]{:S(2)}) %collective-permute-start.17) | collective-permute-done | bytes 114720 | tf_op jit(solution)/shard_map/ppermute | solution.py:442
  105.4 3.4 %collective-permute-done.23.more_ref = f32[64,128]{1,0:T(8,128)S(1)} collective-permute-done((f32[64,128]{1,0:T(8,128)S(1)}, f32[64,128]{1,0:T(8,128)S(1)}, u32[]{:S(2)}, u32[]{:S(2)}) %collective-permute-start.23) | collective-permute-done | bytes 32800 | tf_op jit(solution)/shard_map/ppermute | solution.py:442
  110.4 5.4 %collective-permute-start.25 = (f32[8,128]{1,0:T(8,128)S(1)}, f32[8,128]{1,0:T(8,128)S(1)}, u32[]{:S(2)}, u32[]{:S(2)}) collective-permute-start(f32[8,128]{1,0:T(8,128)S(1)} %get-tuple-element.70), channel_id=1, source_target_pairs={{0,16},{4,20},{8,24},{12,28},{16,0},{20,4},{24,8},{28,12},{1,17},{... | collective-permute-start | bytes 12296 | tf_op jit(solution)/shard_map/ppermute | solution.py:442
  117.4 2.3 %collective-permute-start.26 = (f32[8,128]{1,0:T(8,128)S(1)}, f32[8,128]{1,0:T(8,128)S(1)}, u32[]{:S(2)}, u32[]{:S(2)}) collective-permute-start(f32[8,128]{1,0:T(8,128)S(1)} %add.54), channel_id=1, source_target_pairs={{0,8},{4,12},{8,0},{12,4},{16,24},{20,28},{24,16},{28,20},{1,9},{5... | collective-permute-start | bytes 12296 | tf_op jit(solution)/shard_map/ppermute | solution.py:442
  (71 shorter events, 32.9 us)
Async XLA Ops:
  3.6 8.9 %collective-permute-start = (bf16[72,512]{1,0:T(8,128)(2,1)S(1)}, bf16[72,512]{1,0:T(8,128)(2,1)S(1)}, u32[]{:S(2)}, u32[]{:S(2)}) collective-permute-start(bf16[72,512]{1,0:T(8,128)(2,1)S(1)} %get-tuple-element.38), channel_id=1, source_target_pairs={{0,4},{4,0},{8,12},{12,8},{16,20},{20,16},{24,28},{28,24},{1,5},{5... | collective-permute-start | bytes 221192 | tf_op jit(solution)/shard_map/ppermute | solution.py:442
  6.7 9.5 %collective-permute-start.1 = (bf16[72,512]{1,0:T(8,128)(2,1)S(1)}, bf16[72,512]{1,0:T(8,128)(2,1)S(1)}, u32[]{:S(2)}, u32[]{:S(2)}) collective-permute-start(bf16[72,512]{1,0:T(8,128)(2,1)S(1)} %get-tuple-element.39), channel_id=1, source_target_pairs={{0,8},{4,12},{8,0},{12,4},{16,24},{20,28},{24,16},{28,20},{1,9},{5... | collective-permute-start | bytes 221192 | tf_op jit(solution)/shard_map/ppermute | solution.py:442
  8.3 13.7 %collective-permute-start.2 = (bf16[72,512]{1,0:T(8,128)(2,1)S(1)}, bf16[72,512]{1,0:T(8,128)(2,1)S(1)}, u32[]{:S(2)}, u32[]{:S(2)}) collective-permute-start(bf16[72,512]{1,0:T(8,128)(2,1)S(1)} %get-tuple-element.40), channel_id=1, source_target_pairs={{0,12},{4,8},{8,4},{12,0},{16,28},{20,24},{24,20},{28,16},{1,13},{... | collective-permute-start | bytes 221192 | tf_op jit(solution)/shard_map/ppermute | solution.py:442
  8.3 13.7 %collective-permute-start.3 = (bf16[72,512]{1,0:T(8,128)(2,1)S(1)}, bf16[72,512]{1,0:T(8,128)(2,1)S(1)}, u32[]{:S(2)}, u32[]{:S(2)}) collective-permute-start(bf16[72,512]{1,0:T(8,128)(2,1)S(1)} %get-tuple-element.41), channel_id=1, source_target_pairs={{0,16},{4,20},{8,24},{12,28},{16,0},{20,4},{24,8},{28,12},{1,17},{... | collective-permute-start | bytes 221192 | tf_op jit(solution)/shard_map/ppermute | solution.py:442
  11.3 12.1 %collective-permute-start.4 = (bf16[72,512]{1,0:T(8,128)(2,1)S(1)}, bf16[72,512]{1,0:T(8,128)(2,1)S(1)}, u32[]{:S(2)}, u32[]{:S(2)}) collective-permute-start(bf16[72,512]{1,0:T(8,128)(2,1)S(1)} %get-tuple-element.42), channel_id=1, source_target_pairs={{0,20},{4,16},{8,28},{12,24},{16,4},{20,0},{24,12},{28,8},{1,21},{... | collective-permute-start | bytes 221192 | tf_op jit(solution)/shard_map/ppermute | solution.py:442
  12.6 10.8 %collective-permute-start.5 = (bf16[72,512]{1,0:T(8,128)(2,1)S(1)}, bf16[72,512]{1,0:T(8,128)(2,1)S(1)}, u32[]{:S(2)}, u32[]{:S(2)}) collective-permute-start(bf16[72,512]{1,0:T(8,128)(2,1)S(1)} %get-tuple-element.43), channel_id=1, source_target_pairs={{0,24},{4,28},{8,16},{12,20},{16,8},{20,12},{24,0},{28,4},{1,25},{... | collective-permute-start | bytes 221192 | tf_op jit(solution)/shard_map/ppermute | solution.py:442
  16.2 7.2 %collective-permute-start.6 = (bf16[72,512]{1,0:T(8,128)(2,1)S(1)}, bf16[72,512]{1,0:T(8,128)(2,1)S(1)}, u32[]{:S(2)}, u32[]{:S(2)}) collective-permute-start(bf16[72,512]{1,0:T(8,128)(2,1)S(1)} %get-tuple-element.44), channel_id=1, source_target_pairs={{0,28},{4,24},{8,20},{12,16},{16,12},{20,8},{24,4},{28,0},{1,29},{... | collective-permute-start | bytes 221192 | tf_op jit(solution)/shard_map/ppermute | solution.py:442
  29.3 23.7 %collective-permute-start.8 = (bf16[3,160,1024]{2,1,0:T(8,128)(2,1)S(1)}, bf16[3,160,1024]{2,1,0:T(8,128)(2,1)S(1)}, u32[]{:S(2)}, u32[]{:S(2)}) collective-permute-start(bf16[3,160,1024]{2,1,0:T(8,128)(2,1)S(1)} %preact.5.own_ref), channel_id=1, source_target_pairs={{0,1},{1,0},{2,3},{3,2},{4,5},{5,4},{6,7},{7,6},{8,9},{9,8},{10,11... | collective-permute-start | bytes 2949128 | tf_op jit(solution)/shard_map/ppermute | solution.py:442
  35.3 15.4 %collective-permute-start.9 = (bf16[3,160,1024]{2,1,0:T(8,128)(2,1)S(1)}, bf16[3,160,1024]{2,1,0:T(8,128)(2,1)S(1)}, u32[]{:S(2)}, u32[]{:S(2)}) collective-permute-start(bf16[3,160,1024]{2,1,0:T(8,128)(2,1)S(1)} %preact.6.own_ref), channel_id=1, source_target_pairs={{0,1},{1,0},{2,3},{3,2},{4,5},{5,4},{6,7},{7,6},{8,9},{9,8},{10,11... | collective-permute-start | bytes 2949128 | tf_op jit(solution)/shard_map/ppermute | solution.py:442
  41.8 6.8 %collective-permute-start.10 = (bf16[3,160,1024]{2,1,0:T(8,128)(2,1)S(1)}, bf16[3,160,1024]{2,1,0:T(8,128)(2,1)S(1)}, u32[]{:S(2)}, u32[]{:S(2)}) collective-permute-start(bf16[3,160,1024]{2,1,0:T(8,128)(2,1)S(1)} %preact.7.own_ref), channel_id=1, source_target_pairs={{0,1},{1,0},{2,3},{3,2},{4,5},{5,4},{6,7},{7,6},{8,9},{9,8},{10,11... | collective-permute-start | bytes 2949128 | tf_op jit(solution)/shard_map/ppermute | solution.py:442
  48.0 7.2 %collective-permute-start.7 = (bf16[3,160,1024]{2,1,0:T(8,128)(2,1)S(1)}, bf16[3,160,1024]{2,1,0:T(8,128)(2,1)S(1)}, u32[]{:S(2)}, u32[]{:S(2)}) collective-permute-start(bf16[3,160,1024]{2,1,0:T(8,128)(2,1)S(1)} %preact.4.own_ref), channel_id=1, source_target_pairs={{0,1},{1,0},{2,3},{3,2},{4,5},{5,4},{6,7},{7,6},{8,9},{9,8},{10,11... | collective-permute-start | bytes 2949128 | tf_op jit(solution)/shard_map/ppermute | solution.py:442
  63.0 9.9 %collective-permute-start.11 = (bf16[2,56,1024]{2,1,0:T(8,128)(2,1)S(1)}, bf16[2,56,1024]{2,1,0:T(8,128)(2,1)S(1)}, u32[]{:S(2)}, u32[]{:S(2)}) collective-permute-start(bf16[2,56,1024]{2,1,0:T(8,128)(2,1)S(1)} %get-tuple-element.54), channel_id=1, source_target_pairs={{0,2},{2,0},{1,3},{3,1},{4,6},{6,4},{5,7},{7,5},{8,10},{10,8},{9,1... | collective-permute-start | bytes 688136 | tf_op jit(solution)/shard_map/ppermute | solution.py:442
  64.6 11.9 %collective-permute-start.13 = (bf16[2,56,1024]{2,1,0:T(8,128)(2,1)S(1)}, bf16[2,56,1024]{2,1,0:T(8,128)(2,1)S(1)}, u32[]{:S(2)}, u32[]{:S(2)}) collective-permute-start(bf16[2,56,1024]{2,1,0:T(8,128)(2,1)S(1)} %get-tuple-element.56), channel_id=1, source_target_pairs={{0,2},{2,0},{1,3},{3,1},{4,6},{6,4},{5,7},{7,5},{8,10},{10,8},{9,1... | collective-permute-start | bytes 688136 | tf_op jit(solution)/shard_map/ppermute | solution.py:442
  68.0 13.4 %collective-permute-start.16 = (bf16[2,56,1024]{2,1,0:T(8,128)(2,1)S(1)}, bf16[2,56,1024]{2,1,0:T(8,128)(2,1)S(1)}, u32[]{:S(2)}, u32[]{:S(2)}) collective-permute-start(bf16[2,56,1024]{2,1,0:T(8,128)(2,1)S(1)} %get-tuple-element.62), channel_id=1, source_target_pairs={{0,2},{2,0},{1,3},{3,1},{4,6},{6,4},{5,7},{7,5},{8,10},{10,8},{9,1... | collective-permute-start | bytes 688136 | tf_op jit(solution)/shard_map/ppermute | solution.py:442
  69.6 16.0 %collective-permute-start.19 = (bf16[2,56,1024]{2,1,0:T(8,128)(2,1)S(1)}, bf16[2,56,1024]{2,1,0:T(8,128)(2,1)S(1)}, u32[]{:S(2)}, u32[]{:S(2)}) collective-permute-start(bf16[2,56,1024]{2,1,0:T(8,128)(2,1)S(1)} %get-tuple-element.64), channel_id=1, source_target_pairs={{0,2},{2,0},{1,3},{3,1},{4,6},{6,4},{5,7},{7,5},{8,10},{10,8},{9,1... | collective-permute-start | bytes 688136 | tf_op jit(solution)/shard_map/ppermute | solution.py:442
  73.0 16.5 %collective-permute-start.12 = (bf16[56,1024]{1,0:T(8,128)(2,1)S(1)}, bf16[56,1024]{1,0:T(8,128)(2,1)S(1)}, u32[]{:S(2)}, u32[]{:S(2)}) collective-permute-start(bf16[56,1024]{1,0:T(8,128)(2,1)S(1)} %get-tuple-element.80), channel_id=1, source_target_pairs={{0,4},{4,0},{8,12},{12,8},{16,20},{20,16},{24,28},{28,24},{1,5},{5... | collective-permute-start | bytes 344072 | tf_op jit(solution)/shard_map/ppermute | solution.py:442
  76.6 14.5 %collective-permute-start.15 = (bf16[56,1024]{1,0:T(8,128)(2,1)S(1)}, bf16[56,1024]{1,0:T(8,128)(2,1)S(1)}, u32[]{:S(2)}, u32[]{:S(2)}) collective-permute-start(bf16[56,1024]{1,0:T(8,128)(2,1)S(1)} %get-tuple-element.78), channel_id=1, source_target_pairs={{0,12},{4,8},{8,4},{12,0},{16,28},{20,24},{24,20},{28,16},{1,13},{... | collective-permute-start | bytes 344072 | tf_op jit(solution)/shard_map/ppermute | solution.py:442
  79.8 13.6 %collective-permute-start.14 = (bf16[56,1024]{1,0:T(8,128)(2,1)S(1)}, bf16[56,1024]{1,0:T(8,128)(2,1)S(1)}, u32[]{:S(2)}, u32[]{:S(2)}) collective-permute-start(bf16[56,1024]{1,0:T(8,128)(2,1)S(1)} %get-tuple-element.79), channel_id=1, source_target_pairs={{0,8},{4,12},{8,0},{12,4},{16,24},{20,28},{24,16},{28,20},{1,9},{5... | collective-permute-start | bytes 344072 | tf_op jit(solution)/shard_map/ppermute | solution.py:442
  81.5 11.9 %collective-permute-start.18 = (bf16[56,1024]{1,0:T(8,128)(2,1)S(1)}, bf16[56,1024]{1,0:T(8,128)(2,1)S(1)}, u32[]{:S(2)}, u32[]{:S(2)}) collective-permute-start(bf16[56,1024]{1,0:T(8,128)(2,1)S(1)} %get-tuple-element.76), channel_id=1, source_target_pairs={{0,20},{4,16},{8,28},{12,24},{16,4},{20,0},{24,12},{28,8},{1,21},{... | collective-permute-start | bytes 344072 | tf_op jit(solution)/shard_map/ppermute | solution.py:442
  85.6 14.8 %collective-permute-start.17 = (bf16[56,1024]{1,0:T(8,128)(2,1)S(1)}, bf16[56,1024]{1,0:T(8,128)(2,1)S(1)}, u32[]{:S(2)}, u32[]{:S(2)}) collective-permute-start(bf16[56,1024]{1,0:T(8,128)(2,1)S(1)} %get-tuple-element.77), channel_id=1, source_target_pairs={{0,16},{4,20},{8,24},{12,28},{16,0},{20,4},{24,8},{28,12},{1,17},{... | collective-permute-start | bytes 344072 | tf_op jit(solution)/shard_map/ppermute | solution.py:442
  89.6 10.8 %collective-permute-start.21 = (bf16[56,1024]{1,0:T(8,128)(2,1)S(1)}, bf16[56,1024]{1,0:T(8,128)(2,1)S(1)}, u32[]{:S(2)}, u32[]{:S(2)}) collective-permute-start(bf16[56,1024]{1,0:T(8,128)(2,1)S(1)} %get-tuple-element.74), channel_id=1, source_target_pairs={{0,28},{4,24},{8,20},{12,16},{16,12},{20,8},{24,4},{28,0},{1,29},{... | collective-permute-start | bytes 344072 | tf_op jit(solution)/shard_map/ppermute | solution.py:442
  91.1 9.3 %collective-permute-start.20 = (bf16[56,1024]{1,0:T(8,128)(2,1)S(1)}, bf16[56,1024]{1,0:T(8,128)(2,1)S(1)}, u32[]{:S(2)}, u32[]{:S(2)}) collective-permute-start(bf16[56,1024]{1,0:T(8,128)(2,1)S(1)} %get-tuple-element.75), channel_id=1, source_target_pairs={{0,24},{4,28},{8,16},{12,20},{16,8},{20,12},{24,0},{28,4},{1,25},{... | collective-permute-start | bytes 344072 | tf_op jit(solution)/shard_map/ppermute | solution.py:442
  102.1 6.7 %collective-permute-start.24 = (bf16[64,1024]{1,0:T(8,128)(2,1)S(1)}, bf16[64,1024]{1,0:T(8,128)(2,1)S(1)}, u32[]{:S(2)}, u32[]{:S(2)}) collective-permute-start(bf16[64,1024]{1,0:T(8,128)(2,1)S(1)} %get-tuple-element.67), channel_id=1, source_target_pairs={{0,2},{2,0},{1,3},{3,1},{4,6},{6,4},{5,7},{7,5},{8,10},{10,8},{9,1... | collective-permute-start | bytes 393224 | tf_op jit(solution)/shard_map/ppermute | solution.py:442
  110.4 7.0 %collective-permute-start.25 = (f32[8,128]{1,0:T(8,128)S(1)}, f32[8,128]{1,0:T(8,128)S(1)}, u32[]{:S(2)}, u32[]{:S(2)}) collective-permute-start(f32[8,128]{1,0:T(8,128)S(1)} %get-tuple-element.70), channel_id=1, source_target_pairs={{0,16},{4,20},{8,24},{12,28},{16,0},{20,4},{24,8},{28,12},{1,17},{... | collective-permute-start | bytes 12296 | tf_op jit(solution)/shard_map/ppermute | solution.py:442
  (10 other events, 189.6 us)
